TPU v7x, 32 devices: a whole 2x2x4 slice. The times are simulated.
32 devices in a mesh: grp: 4 (over y, core), dom: 8 (over z, x).
Axes of the slice: x: 2, y: 2, z: 4, core: 2. Of those that a mesh axis runs over, the one named last changes fastest.
Arguments:
- element_state: float32 [56, 9, 20480], P(None, None, ('grp', 'dom')), may hold values from -6 to 6
- stiffness: float32 [3, 56, 56], replicated, may hold values from -0.75 to 0.75
- flux_local: float32 [4, 56, 56], replicated, may hold values from -0.75 to 0.75
- flux_remote: float32 [4, 56, 56], replicated, may hold values from -0.75 to 0.75
- star_matrix: float32 [3, 9, 9, 20480], P(None, None, None, ('grp', 'dom')), may hold values from -0.18 to 0.18
- face_local: float32 [4, 9, 9, 20480], P(None, None, None, ('grp', 'dom')), may hold values from -0.15 to 0.15
- face_remote: float32 [4, 9, 9, 20480], P(None, None, None, ('grp', 'dom')), may hold values from -0.15 to 0.15
- energy_weight: float32 [9, 20480], P(None, ('grp', 'dom')), may hold values from 0.5 to 18
- face_neighbour: int32 [4, 20480], P(None, ('grp', 'dom')), may hold values from 0 to 1151, as said below
- element_count: int32 [32], P(('grp', 'dom')), may hold values from 160 to 640, as said below
- send_count: int32 [32, 8], P(('grp', 'dom')), may hold values from 0 to 64, as said below
- send_element: int32 [32, 8, 64], P(('grp', 'dom')), may hold values from 0 to 639, as said below
- receiver_element: int32 [512], P(('grp', 'dom')), may hold values from 0 to 639, as said below
- receiver_slot: int32 [512], P(('grp', 'dom')), may hold values from 0 to 127, as said below
- receiver_weight: float32 [56, 512], P(None, ('grp', 'dom')), may hold values from -0.75 to 0.75
Outputs:
- new_state: float32 [56, 9, 20480], P(None, None, ('grp', 'dom'))
- energy: float32 [4, 3], P('grp')
- traces: float32 [3, 9, 512], P(None, None, ('grp', 'dom'))
Inputs may be any that keep to these rules, and one draw needn't show every extreme that they name: The first element_count[p] slots of a partition are active. In every slab 4 partitions in a row along dom (cyclically) hold 640 active elements; the others hold from 160 to 320. `send_count`: every partition has exactly 64 in one of its first 6 slots. `send_element`: names active elements of the sending partition. `face_neighbour`: values below 640 name active elements of the partition itself. `receiver_element`: names an active element of the owning partition. `receiver_slot`: within each slab a permutation of the 128 rows.
All inputs are finite; a program needn't handle non-finite values.
Results may differ from a plain program's by a relative error of at most 0.0001.
Values sent between devices are 32-bit elements; how exact they have to be, the bound alone decides.
A program may use at most 128 MiB of HBM per device.

v0:
```python
import functools

import jax
import jax.numpy as jnp
from jax import lax
from jax.experimental import pallas as pl
from jax.experimental.pallas import tpu as pltpu
from jax.sharding import PartitionSpec as P

PEER_REACH = 3
TIME_STEPS = 3
LANES = 128


def one_hot(rows, names):
    place = lax.broadcasted_iota(jnp.int32, (rows, names.shape[1]), 0)
    return jnp.where(place == names, 1.0, 0.0).astype(jnp.bfloat16)


def dot(a, b):
    return jnp.dot(a, b, preferred_element_type=jnp.float32)


def stacked_matrix(matrices):
    high = lax.reduce_precision(matrices, 8, 7)
    low = (matrices - high).astype(jnp.bfloat16)
    high = high.astype(jnp.bfloat16)
    return jnp.concatenate([high, high, low, low], 2)


def row_chunks(rows):
    middle = min(rows, 32)
    return [(0, middle), (middle, rows)] if middle < rows else [(0, rows)]


def split_rows(field):
    high = field.astype(jnp.bfloat16).astype(jnp.float32)
    return jnp.concatenate([high, field - high], 0).astype(jnp.bfloat16)


def pack_kernel(top, x_ref, names_ref, weight_ref, rec_ref, gains_ref, msg_ref, split_ref, value_ref, energy_ref, taken):
    quantities, basis, elements = x_ref.shape
    width = 2 * LANES
    total = jnp.zeros((1, elements), jnp.float32)
    for q in range(quantities):
        field = x_ref[q]
        total = total + gains_ref[q : q + 1, :] * jnp.sum(field * field, axis=0, keepdims=True)
        split_ref[2 * q * basis : 2 * (q + 1) * basis, :] = split_rows(field)
    energy_ref[...] = total
    picked = dot(split_ref[...], one_hot(elements, rec_ref[...]))
    for q in range(quantities):
        start = 2 * q * basis
        here = picked[start : start + basis] + picked[start + basis : start + 2 * basis]
        value_ref[q : q + 1, :] = jnp.sum(here * weight_ref[...], axis=0, keepdims=True)
    half = LANES // 2
    lane = lax.broadcasted_iota(jnp.int32, (basis, LANES), 1)
    for start_lane in range(0, names_ref.shape[1], width):
        taken[...] = dot(split_ref[...], one_hot(elements, names_ref[:, start_lane : start_lane + width]))
        for part in range(width // LANES):
            slot = 2 * (start_lane // LANES + part)
            lanes = slice(part * LANES, (part + 1) * LANES)

            def of(q):
                start = 2 * q * basis
                return taken[start : start + basis, lanes] + taken[start + basis : start + 2 * basis, lanes]

            for q in range(top):
                rows = slice(q * basis, (q + 1) * basis)
                upper = of(q)
                lower = of(q + top) if q + top < quantities else upper
                msg_ref[slot, rows, :] = jnp.where(lane < half, upper, pltpu.roll(lower, half, 1))
                msg_ref[slot + 1, rows, :] = jnp.where(lane < half, pltpu.roll(upper, half, 1), lower)


def halo_ways(slot_number):
    if slot_number < PEER_REACH:
        return "dom", slot_number + 1
    if slot_number < 2 * PEER_REACH:
        return "dom", PEER_REACH - 1 - slot_number
    return "grp", 1 if slot_number == 2 * PEER_REACH else -1


def peer(axis, by):
    place = lax.axis_index(axis)
    count = lax.axis_size(axis)
    if axis == "dom":
        return {axis: lax.rem(place + by + count, count)}, None
    other = place + by
    return {axis: jnp.clip(other, 0, count - 1)}, (other >= 0) & (other < count)


def guarded(condition, action):
    if condition is None:
        action()
    else:
        pl.when(condition)(action)


def local_kernel(x_ref, matrix_ref, star_ref, face_ref, msg_ref, out_ref, halo_ref, held, terms, send_sem, recv_sem):
    quantities, basis, elements = x_ref.shape
    slots = msg_ref.shape[0]
    star_total, face_total = star_ref.shape[2], face_ref.shape[2]
    barrier = pltpu.get_barrier_semaphore()
    ways = [halo_ways(slot) for slot in range(slots)]
    for way in ways:
        device, there = peer(*way)
        guarded(
            there,
            lambda: pl.semaphore_signal(barrier, inc=1, device_id=device, device_id_type=pl.DeviceIdType.MESH),
        )
    greeted = 0
    for way in ways:
        _, there = peer(*way)
        greeted = greeted + (1 if there is None else there.astype(jnp.int32))
    pl.semaphore_wait(barrier, greeted)

    def copy(slot):
        device, there = peer(*ways[slot])
        return (
            pltpu.make_async_remote_copy(
                src_ref=msg_ref.at[slot],
                dst_ref=held.at[slot],
                send_sem=send_sem.at[slot],
                recv_sem=recv_sem.at[slot],
                device_id=device,
                device_id_type=pl.DeviceIdType.MESH,
            ),
            there,
        )

    for slot in range(slots):
        sent, there = copy(slot)
        guarded(there, sent.start)

    def one_block(number, carry):
        lanes = pl.ds(pl.multiple_of(number * LANES, LANES), LANES)

        for q in range(quantities):
            both = split_rows(x_ref[q, :, lanes])
            terms[q] = dot(matrix_ref[...], jnp.concatenate([both, both], 0))
        for first, last in row_chunks(basis):

            def one_quantity(q, sums):
                for n in range(star_total + face_total):
                    ref, at = (star_ref, n) if n < star_total else (face_ref, n - star_total)
                    term = terms[q, n * basis + first : n * basis + last, :]
                    sums = sums + ref[:, q, at : at + 1, lanes] * term[None]
                return sums

            start = jnp.zeros((quantities, last - first, LANES), jnp.float32)
            out_ref[:, first:last, lanes] = lax.fori_loop(0, quantities, one_quantity, start)
        return carry

    lax.fori_loop(0, elements // LANES, one_block, 0)
    for slot in range(slots):
        sent, there = copy(slot)
        guarded(there, sent.wait_send)
        axis, by = ways[slot]
        _, came = peer(axis, -by)

        def take(sent=sent, slot=slot):
            sent.wait_recv()
            halo_ref[slot] = held[slot]

        guarded(came, take)
        if came is not None:

            @pl.when(jnp.logical_not(came))
            def _(slot=slot):
                halo_ref[slot] = jnp.zeros(held.shape[1:], jnp.float32)


def remote_kernel(top, x_ref, part_ref, split_ref, matrix_ref, face_ref, names_ref, live_ref, halo_ref, out_ref, wide, *scratch):
    quantities, basis, width = x_ref.shape
    elements = split_ref.shape[1]
    faces = face_ref.shape[2]
    slots = halo_ref.shape[0]
    half = LANES // 2

    @pl.when(pl.program_id(0) == 0)
    def _():
        wide[:, :elements] = split_ref[...]
        lane = lax.broadcasted_iota(jnp.int32, (basis, LANES), 1)
        for pair in range(slots // 2):
            lanes = slice(elements + pair * LANES, elements + (pair + 1) * LANES)
            for q in range(quantities):
                at = q if q < top else q - top
                rows = slice(at * basis, (at + 1) * basis)
                even, odd = halo_ref[2 * pair, rows, :], halo_ref[2 * pair + 1, rows, :]
                if q < top:
                    value = jnp.where(lane < half, even, pltpu.roll(odd, half, 1))
                else:
                    value = jnp.where(lane < half, pltpu.roll(even, half, 1), odd)
                wide[2 * q * basis : 2 * (q + 1) * basis, lanes] = split_rows(value)

    pairs = faces // 2
    picked, terms = scratch[:pairs], scratch[pairs : 2 * pairs]
    for pair in range(pairs):
        hot = jnp.concatenate(
            [one_hot(wide.shape[1], names_ref[f : f + 1, :]) for f in (2 * pair, 2 * pair + 1)], 1
        )
        picked[pair][...] = dot(wide[...], hot).astype(jnp.bfloat16)
        for q in range(quantities):
            for f in range(2):
                both = picked[pair][2 * q * basis : 2 * (q + 1) * basis, f * width : (f + 1) * width]
                terms[pair][q, f * basis : (f + 1) * basis, :] = dot(
                    matrix_ref[2 * pair + f], jnp.concatenate([both, both], 0)
                )
    live = live_ref[...] > 0.5
    for first, last in row_chunks(basis):
        sums = [jnp.zeros((last - first, width), jnp.float32) for _ in range(quantities)]
        for f in range(faces):
            for q in range(quantities):
                term = terms[f // 2][q, f % 2 * basis + first : f % 2 * basis + last, :]
                for p in range(quantities):
                    sums[p] = sums[p] + face_ref[p, q, f : f + 1, :] * term
        for p in range(quantities):
            field = x_ref[p, first:last, :]
            out_ref[p, first:last, :] = jnp.where(live, field + (part_ref[p, first:last, :] - sums[p]), field)


def gather_kernel(axis, table_ref, all_ref, held, send_sem, recv_sem):
    count = lax.axis_size(axis)
    me = lax.axis_index(axis)
    barrier = pltpu.get_barrier_semaphore()

    def other(step):
        return lax.rem(me + step, count)

    def greet(step, carry):
        pl.semaphore_signal(
            barrier, inc=1, device_id={axis: other(step)}, device_id_type=pl.DeviceIdType.MESH
        )
        return carry

    lax.fori_loop(1, count, greet, 0)
    pl.semaphore_wait(barrier, count - 1)

    def copy(step, slot):
        return pltpu.make_async_remote_copy(
            src_ref=table_ref,
            dst_ref=held.at[slot],
            send_sem=send_sem.at[step],
            recv_sem=recv_sem.at[slot],
            device_id={axis: other(step)},
            device_id_type=pl.DeviceIdType.MESH,
        )

    def start(step, carry):
        copy(step, me).start()
        return carry

    lax.fori_loop(1, count, start, 0)

    def finish(step, carry):
        copy(step, me).wait_send()
        source = other(step)
        copy(step, source).wait_recv()
        all_ref[source] = held[source]
        return carry

    lax.fori_loop(1, count, finish, 0)
    all_ref[me] = table_ref[...]


def per_device(
    element_state,
    stiffness,
    flux_local,
    flux_remote,
    star_matrix,
    face_local,
    face_remote,
    energy_weight,
    face_neighbour,
    element_count,
    send_count,
    send_element,
    receiver_element,
    receiver_slot,
    receiver_weight,
):
    basis, quantities, elements = element_state.shape
    slots, capacity = send_element.shape[1:]
    receivers = receiver_slot.shape[0]
    dimensions, faces = stiffness.shape[0], flux_local.shape[0]
    group_size = lax.axis_size("dom")
    top = (quantities + 1) // 2
    f32, bf16 = jnp.float32, jnp.bfloat16
    width = LANES
    blocks = elements // width

    local_matrix = stacked_matrix(jnp.concatenate([stiffness, -flux_local], 0))
    local_matrix = local_matrix.reshape(-1, local_matrix.shape[2])
    remote_matrix = stacked_matrix(flux_remote)
    slot_live = jnp.arange(capacity)[None, :] < send_count[0][:, None]
    names = jnp.where(slot_live, send_element[0], -1).reshape(1, -1)
    rec_names = jnp.pad(receiver_element[None, :], ((0, 0), (0, LANES - receivers)), constant_values=-1)
    rec_weight = jnp.pad(receiver_weight, ((0, 0), (0, LANES - receivers)))
    live = (jnp.arange(elements)[None, :] < element_count[0]).astype(f32)
    gains = energy_weight * live
    fields = jnp.transpose(element_state, (1, 0, 2))
    stars = jnp.transpose(star_matrix, (1, 2, 0, 3))
    near = jnp.transpose(face_local, (1, 2, 0, 3))
    far = jnp.transpose(face_remote, (1, 2, 0, 3))

    pack = pl.pallas_call(
        functools.partial(pack_kernel, top),
        out_shape=(
            jax.ShapeDtypeStruct((slots, top * basis, LANES), f32),
            jax.ShapeDtypeStruct((2 * quantities * basis, elements), bf16),
            jax.ShapeDtypeStruct((quantities, LANES), f32),
            jax.ShapeDtypeStruct((1, elements), f32),
        ),
        scratch_shapes=[pltpu.VMEM((2 * quantities * basis, 2 * LANES), f32)],
        compiler_params=pltpu.CompilerParams(vmem_limit_bytes=40 << 20),
        cost_estimate=pl.CostEstimate(flops=2_000_000_000, bytes_accessed=5_000_000, transcendentals=0),
        name="pack",
    )
    block = pl.BlockSpec((quantities, basis, width), lambda i: (0, 0, i))

    def whole(array):
        rank = len(array.shape)
        return pl.BlockSpec(array.shape, lambda i: (0,) * rank)

    def coefficients(array):
        return pl.BlockSpec(array.shape[:3] + (width,), lambda i: (0, 0, 0, i))

    state = jax.ShapeDtypeStruct((quantities, basis, elements), f32)
    mail = jax.ShapeDtypeStruct((slots, top * basis, LANES), f32)
    in_vmem = pl.BlockSpec(memory_space=pltpu.VMEM)
    local = pl.pallas_call(
        local_kernel,
        out_shape=(state, mail),
        in_specs=[in_vmem] * 5,
        out_specs=(in_vmem, in_vmem),
        scratch_shapes=[
            pltpu.VMEM(mail.shape, f32),
            pltpu.VMEM((quantities, local_matrix.shape[0], width), f32),
            pltpu.SemaphoreType.DMA((slots,)),
            pltpu.SemaphoreType.DMA((slots,)),
        ],
        compiler_params=pltpu.CompilerParams(
            vmem_limit_bytes=40 << 20, collective_id=0, has_side_effects=True
        ),
        name="local",
    )
    split_shape = jax.ShapeDtypeStruct((2 * quantities * basis, elements), bf16)
    remote = pl.pallas_call(
        functools.partial(remote_kernel, top),
        out_shape=state,
        grid=(blocks,),
        in_specs=[
            block,
            block,
            whole(split_shape),
            whole(remote_matrix),
            coefficients(far),
            pl.BlockSpec((faces, width), lambda i: (0, i)),
            pl.BlockSpec((1, width), lambda i: (0, i)),
            whole(mail),
        ],
        out_specs=block,
        scratch_shapes=[
            pltpu.VMEM((2 * quantities * basis, elements + slots * capacity), bf16),
        ]
        + [pltpu.VMEM((2 * quantities * basis, 2 * width), bf16)] * (faces // 2)
        + [pltpu.VMEM((quantities, 2 * basis, width), f32)] * (faces // 2),
        compiler_params=pltpu.CompilerParams(vmem_limit_bytes=40 << 20),
        cost_estimate=pl.CostEstimate(flops=8_000_000_000, bytes_accessed=6_000_000, transcendentals=0),
        name="remote",
    )

    values = []
    energies = []
    messages, halves, _, _ = pack(fields, names, rec_weight, rec_names, gains)
    for time_step in range(TIME_STEPS):
        partial, halo = local(fields, local_matrix, stars, near, messages)
        fields = remote(fields, partial, halves, remote_matrix, far, face_neighbour, live, halo)
        messages, halves, value, energy = pack(fields, names, rec_weight, rec_names, gains)
        values.append(value)
        energies.append(energy)
    own_energy = 0.5 * jnp.sum(jnp.concatenate(energies, 0), axis=1)
    slot_row = receiver_slot.astype(f32)[None, :]
    table = jnp.concatenate(
        [
            jnp.concatenate(values, 0)[:, :receivers],
            slot_row,
            jnp.broadcast_to(own_energy[:, None], (TIME_STEPS, receivers)),
        ],
        0,
    )
    rows = (table.shape[0] + 7) // 8 * 8
    table = jnp.pad(table, ((0, rows - table.shape[0]), (0, LANES - receivers)))
    everyone = pl.pallas_call(
        functools.partial(gather_kernel, "dom"),
        out_shape=jax.ShapeDtypeStruct((group_size, rows, LANES), f32),
        in_specs=[in_vmem],
        out_specs=in_vmem,
        scratch_shapes=[
            pltpu.VMEM((group_size, rows, LANES), f32),
            pltpu.SemaphoreType.DMA((group_size,)),
            pltpu.SemaphoreType.DMA((group_size,)),
        ],
        compiler_params=pltpu.CompilerParams(collective_id=1, has_side_effects=True),
        name="gather",
    )(table)[:, :, :receivers]
    count = TIME_STEPS * quantities
    mine = (lax.axis_index("dom") * receivers + jnp.arange(receivers)).astype(f32)
    matches = (everyone[:, count, :, None] == mine).astype(f32)
    traces = jnp.einsum(
        "dkr,drs->ks", everyone[:, :count], matches, precision=lax.Precision.HIGHEST, preferred_element_type=f32
    )
    denominator = float(group_size * elements * basis * quantities)
    energy = jnp.sum(everyone[:, count + 1 : count + 1 + TIME_STEPS, 0], axis=0) / denominator
    return (
        jnp.transpose(fields, (1, 0, 2)),
        energy[None, :],
        traces.reshape(TIME_STEPS, quantities, receivers),
    )


def solution(mesh):
    both = ("grp", "dom")
    return jax.shard_map(
        per_device,
        mesh=mesh,
        in_specs=(
            P(None, None, both),
            P(),
            P(),
            P(),
            P(None, None, None, both),
            P(None, None, None, both),
            P(None, None, None, both),
            P(None, both),
            P(None, both),
            P(both),
            P(both, None),
            P(both, None, None),
            P(both),
            P(both),
            P(None, both),
        ),
        out_specs=(P(None, None, both), P("grp", None), P(None, None, both)),
        check_vma=False,
    )
```

profile of v0, /device:TPU:0, one launch (start us, length us, event | category | flops | bytes accessed | tf_op | source)
XLA Modules:
  0.0 163.6 jit_solution(8395632838160596460)
XLA Ops:
  1.3 0.8 broadcast_multiply_fusion.gains_ref
  2.1 0.8 copy.21
  2.9 0.7 iota_compare_fusion.1
  3.6 0.1 lt.48
  3.7 0.8 squeeze.7
  4.4 0.7 pad.13.rec_ref
  5.1 0.0 copy-start.2
  5.1 1.3 copy-done.2
  6.4 0.0 copy-start.6
  6.4 0.0 copy-start.8
  6.4 0.0 copy-start.1
  6.4 2.1 %pack.4 = (f32[8,280,128]{2,1,0:T(8,128)S(1)}, bf16[1008,640]{1,0:T(8,128)(2,1)S(1)}, f32[9,128]{1,0:T(8,128)}, f32[1,640]{1,0:T(1,128)}) custom-call(f32[9,56,640]{2,1,0:T(8,128)S(1)} %bitcast.26, s32[1,512]{1,0:T(1,128)S(1)} %broadcast_select_fusion.names_ref, f32[56,128]{1,0:T(8,128)S(1)} %pad.12.weight_ref, s32[1,128]{1,0:T(1,128)S(1)} %pad.13.rec_ref, ...), custom_call_target="tpu_custom_call" | custom-call | flops 2000000000 | bytes 5000000 | tf_op jit(solution)/shard_map/pack/pallas_call | solution.py:376
  8.6 0.0 copy-start
  8.6 0.0 copy-done.6
  8.6 0.0 copy-done.8
  8.7 0.2 pad_maximum_fusion.1.matrix_ref
  8.9 0.0 copy-done.1
  8.9 0.8 copy-done
  9.7 0.0 copy-start.7
  9.7 0.0 copy-start.3
  9.7 0.0 copy-start.4
  9.7 22.5 %local.3 = (f32[9,56,640]{2,1,0:T(8,128)S(1)}, f32[8,280,128]{2,1,0:T(8,128)S(1)}) custom-call(f32[9,56,640]{2,1,0:T(8,128)S(1)} %bitcast.27, bf16[392,224]{1,0:T(8,128)(2,1)S(1)} %pad_maximum_fusion.1.matrix_ref, f32[9,9,3,640]{3,2,1,0:T(4,128)S(1)} %bitcast.20, f32[9,9,4,640]{3,2,1,0:T(4,128)S(1)} %bitcast.23, f32[8,280,128]{2,1,0:T(8,128)S(1)} %get-tuple-element.21.msg_ref), custom_call_target="tpu_custom_call" | custom-call | tf_op jit(solution)/shard_map/local/pallas_call | solution.py:378
  32.2 0.0 copy-done.7
  32.3 0.1 pad_maximum_fusion.2.matrix_ref
  32.4 0.0 copy-done.3
  32.4 0.0 copy-done.4
  32.5 20.9 %remote.3.x_ref = f32[9,56,640]{2,1,0:T(8,128)S(1)} custom-call(f32[9,56,640]{2,1,0:T(8,128)S(1)} %bitcast.28, f32[9,56,640]{2,1,0:T(8,128)S(1)} %get-tuple-element.22.part_ref, bf16[1008,640]{1,0:T(8,128)(2,1)S(1)} %get-tuple-element.23.split_ref, bf16[4,56,224]{2,1,0:T(8,128)(2,1)S(1)} %pad_maximum_fusion.2.matrix_ref, f32[9,9,4,640]{3,2,1,0:T(4,128)S(1)} %bitcast.29, ...), custom_call_target="tpu_custom_call" | custom-call | flops 8000000000 | bytes 6000000 | tf_op jit(solution)/shard_map/remote/pallas_call | solution.py:379
  53.4 1.5 pack.5
  54.9 22.4 %local.4 = (f32[9,56,640]{2,1,0:T(8,128)S(1)}, f32[8,280,128]{2,1,0:T(8,128)S(1)}) custom-call(f32[9,56,640]{2,1,0:T(8,128)S(1)} %remote.3.x_ref, bf16[392,224]{1,0:T(8,128)(2,1)S(1)} %pad_maximum_fusion.1.matrix_ref, f32[9,9,3,640]{3,2,1,0:T(4,128)S(1)} %bitcast.21, f32[9,9,4,640]{3,2,1,0:T(4,128)S(1)} %bitcast.24, f32[8,280,128]{2,1,0:T(8,128)S(1)} %get-tuple-element.25.msg_ref), custom_call_target="tpu_custom_call" | custom-call | tf_op jit(solution)/shard_map/local/pallas_call | solution.py:378
  77.3 20.9 %remote.4.x_ref = f32[9,56,640]{2,1,0:T(8,128)S(1)} custom-call(f32[9,56,640]{2,1,0:T(8,128)S(1)} %remote.3.x_ref, f32[9,56,640]{2,1,0:T(8,128)S(1)} %get-tuple-element.26.part_ref, bf16[1008,640]{1,0:T(8,128)(2,1)S(1)} %get-tuple-element.27.split_ref, bf16[4,56,224]{2,1,0:T(8,128)(2,1)S(1)} %pad_maximum_fusion.2.matrix_ref, f32[9,9,4,640]{3,2,1,0:T(4,128)S(1)} %bitcast.30, ...), custom_call_target="tpu_custom_call" | custom-call | flops 8000000000 | bytes 6000000 | tf_op jit(solution)/shard_map/remote/pallas_call | solution.py:379
  98.2 1.5 pack.6
  99.7 22.3 %local.5 = (f32[9,56,640]{2,1,0:T(8,128)S(1)}, f32[8,280,128]{2,1,0:T(8,128)S(1)}) custom-call(f32[9,56,640]{2,1,0:T(8,128)S(1)} %remote.4.x_ref, bf16[392,224]{1,0:T(8,128)(2,1)S(1)} %pad_maximum_fusion.1.matrix_ref, f32[9,9,3,640]{3,2,1,0:T(4,128)S(1)} %bitcast.22, f32[9,9,4,640]{3,2,1,0:T(4,128)S(1)} %bitcast.25, f32[8,280,128]{2,1,0:T(8,128)S(1)} %get-tuple-element.29.msg_ref), custom_call_target="tpu_custom_call" | custom-call | tf_op jit(solution)/shard_map/local/pallas_call | solution.py:378
  122.0 21.6 %remote.5.x_ref = f32[9,56,640]{2,1,0:T(8,128)} custom-call(f32[9,56,640]{2,1,0:T(8,128)S(1)} %remote.4.x_ref, f32[9,56,640]{2,1,0:T(8,128)S(1)} %get-tuple-element.30.part_ref, bf16[1008,640]{1,0:T(8,128)(2,1)S(1)} %get-tuple-element.31.split_ref, bf16[4,56,224]{2,1,0:T(8,128)(2,1)S(1)} %pad_maximum_fusion.2.matrix_ref, f32[9,9,4,640]{3,2,1,0:T(4,128)S(1)} %bitcast.31, ...), custom_call_target="tpu_custom_call" | custom-call | flops 8000000000 | bytes 6000000 | tf_op jit(solution)/shard_map/remote/pallas_call | solution.py:379
  143.6 0.0 copy-start.5
  143.6 1.3 copy-done.5
  144.9 0.0 copy-start.9
  144.9 2.5 %pack.7 = (f32[8,280,128]{2,1,0:T(8,128)}, bf16[1008,640]{1,0:T(8,128)(2,1)}, f32[9,128]{1,0:T(8,128)S(1)}, f32[1,640]{1,0:T(1,128)S(1)}) custom-call(f32[9,56,640]{2,1,0:T(8,128)S(1)} %copy-done.5, s32[1,512]{1,0:T(1,128)S(1)} %broadcast_select_fusion.names_ref, f32[56,128]{1,0:T(8,128)S(1)} %pad.12.weight_ref, s32[1,128]{1,0:T(1,128)S(1)} %pad.13.rec_ref, ...), custom_call_target="tpu_custom_call" | custom-call | flops 2000000000 | bytes 5000000 | tf_op jit(solution)/shard_map/pack/pallas_call | solution.py:380
  147.4 0.1 maximum_reduce_fusion
  147.6 0.1 pad.17.clone
  147.7 0.0 copy-done.9
  147.7 0.1 fusion.7
  147.7 0.6 pad.14.table_ref
  148.4 11.2 %gather.1 = f32[8,32,128]{2,1,0:T(8,128)} custom-call(f32[32,128]{1,0:T(8,128)} %pad.14.table_ref), custom_call_target="tpu_custom_call" | custom-call | tf_op jit(solution)/shard_map/gather/pallas_call | solution.py:395
  159.6 0.8 slice.19
  160.4 1.2 convolution_bitcast_fusion
  161.5 0.6 copy.24
  162.2 0.9 slice_reduce_fusion
  163.0 0.5 multiply_bitcast_fusion
  (12 shorter events, 0.1 us)
Async XLA Ops:
  5.1 1.3 copy-start.2
  6.4 2.1 %copy-start.6 = (f32[4,56,56]{2,1,0:T(8,128)S(1)}, f32[4,56,56]{2,1,0:T(8,128)}, u32[]{:S(2)}) copy-start(f32[4,56,56]{2,1,0:T(8,128)} %param.17) | copy-start | bytes 150532
  6.4 2.2 %copy-start.8 = (f32[3,56,56]{2,1,0:T(8,128)S(1)}, f32[3,56,56]{2,1,0:T(8,128)}, u32[]{:S(2)}) copy-start(f32[3,56,56]{2,1,0:T(8,128)} %param.16) | copy-start | bytes 112900
  6.4 2.4 %copy-start.1 = (f32[4,9,9,640]{3,0,2,1:T(4,128)S(1)}, f32[4,9,9,640]{3,0,2,1:T(4,128)}, u32[]{:S(2)}) copy-start(f32[4,9,9,640]{3,0,2,1:T(4,128)} %param.20) | copy-start | bytes 2488324
  8.6 1.1 copy-start
  9.7 22.5 %copy-start.7 = (f32[4,56,56]{2,1,0:T(8,128)S(1)}, f32[4,56,56]{2,1,0:T(8,128)}, u32[]{:S(2)}) copy-start(f32[4,56,56]{2,1,0:T(8,128)} %param.18) | copy-start | bytes 150532
  9.7 22.7 %copy-start.3 = (f32[4,9,9,640]{3,0,2,1:T(4,128)S(1)}, f32[4,9,9,640]{3,0,2,1:T(4,128)}, u32[]{:S(2)}) copy-start(f32[4,9,9,640]{3,0,2,1:T(4,128)} %param.21) | copy-start | bytes 2488324
  9.7 22.7 %copy-start.4 = (s32[4,640]{1,0:T(4,128)S(1)}, s32[4,640]{1,0:T(4,128)}, u32[]{:S(2)}) copy-start(s32[4,640]{1,0:T(4,128)} %names_ref.5) | copy-start | bytes 30724
  143.6 1.3 copy-start.5
  144.9 2.7 %copy-start.9 = (s32[16]{0:T(128)S(1)}, s32[16]{0:T(128)}, u32[]{:S(2)}) copy-start(s32[16]{0:T(128)} %param.28) | copy-start | bytes 196
where the time goes:
time: 164 us
  Pallas kernels  150 us (91%)
  local copies, waits for them, and re-layouts  7.84 us (5%)
  other arithmetic  3.58 us (2%)
    pallas_call x3, Pallas kernels, per_device(): partial, halo = local(fields, local_matrix, stars, near, messages)  67.2 us
    pallas_call x3, Pallas kernels, per_device(): remote(fields, partial, halves, remote_matrix, far, face_neighbour, live,...  63.4 us
    pallas_call x1, Pallas kernels, per_device(): pl.pallas_call(functools.partial(gather_kernel, 'dom'), out_shape=jax.Sha...  11.2 us
    pallas_call x3, Pallas kernels, per_device(): pack(fields, names, rec_weight, rec_names, gains)  5.54 us
    unnamed x22, local copies, waits for them, and re-layouts  4.86 us

commit v1 on v0

v1 whole, which is shorter than its diff:
```python
import functools

import jax
import jax.numpy as jnp
from jax import lax
from jax.experimental import pallas as pl
from jax.experimental.pallas import tpu as pltpu
from jax.sharding import PartitionSpec as P

PEER_REACH = 3
TIME_STEPS = 3
LANES = 128
NEAR = (0, PEER_REACH, 2 * PEER_REACH, 2 * PEER_REACH + 1)
FAR = tuple(s for n in range(1, PEER_REACH) for s in (n, PEER_REACH + n))
ORDER = NEAR + FAR
MESH = pl.DeviceIdType.MESH
f32, bf16 = jnp.float32, jnp.bfloat16


def dot(a, b):
    return jnp.dot(a, b, preferred_element_type=f32)


def halves(field):
    high = field.astype(bf16)
    return high, (field - high.astype(f32)).astype(bf16)


def stacked_rows(field):
    high = field.astype(bf16).astype(f32)
    both = jnp.concatenate([high, field - high], 0).astype(bf16)
    return jnp.concatenate([both, both], 0)


def stacked_matrix(matrices):
    high = lax.reduce_precision(matrices, 8, 7)
    low = (matrices - high).astype(bf16)
    high = high.astype(bf16)
    return jnp.concatenate([high, high, low, low], 2)


def row_chunks(rows):
    middle = min(rows, 32)
    return [(0, middle), (middle, rows)] if middle < rows else [(0, rows)]


def halo_ways(slot_number):
    if slot_number < PEER_REACH:
        return "dom", slot_number + 1
    if slot_number < 2 * PEER_REACH:
        return "dom", PEER_REACH - 1 - slot_number
    return "grp", 1 if slot_number == 2 * PEER_REACH else -1


def peer(axis, by):
    place = lax.axis_index(axis)
    count = lax.axis_size(axis)
    if axis == "dom":
        return {axis: lax.rem(place + by + count, count)}, None
    other = place + by
    return {axis: jnp.clip(other, 0, count - 1)}, (other >= 0) & (other < count)


def guarded(condition, action):
    if condition is None:
        action()
    else:
        pl.when(condition)(action)


def hot_of(first, rows, names):
    place = lax.broadcasted_iota(jnp.int32, (rows, names.shape[1]), 0) + first
    return jnp.where(place == names, 1.0, 0.0).astype(bf16)


def steps_kernel(
    x_hbm, star_hbm, near_hbm, far_hbm,
    mats_ref, weight_ref, faces_ref, names_ref, gains_ref, recs_ref, count_ref,
    out_ref, energy_ref, trace_ref,
    star_ref, near_ref, far_ref, both, cat, terms, part, tcat, rterm, hs, th,
    hot_own, hot_halo, hot_up, hot_low, hot_rec, msg, held, mine, tabs,
    load_sem, send_sem, recv_sem, table_send, table_recv,
):
    quantities, basis, elements = out_ref.shape
    rows = quantities * basis
    slots = msg.shape[0]
    half = LANES // 2
    upper = msg.shape[1]
    lower = rows - upper
    faces = far_ref.shape[2]
    dims = star_ref.shape[2]
    own_rows = (dims + faces) * basis
    group = slots // 2 * half
    steps = TIME_STEPS
    size = lax.axis_size("dom")
    me = lax.axis_index("dom")
    receivers = trace_ref.shape[2]
    ways = [halo_ways(slot) for slot in range(slots)]

    barrier = pltpu.get_barrier_semaphore()

    def dom_other(step):
        return {"dom": lax.rem(me + step, size)}

    def greet(step, carry):
        pl.semaphore_signal(barrier, inc=1, device_id=dom_other(step), device_id_type=MESH)
        return carry

    lax.fori_loop(1, size, greet, 0)
    greeted = size - 1
    for axis, by in ways:
        if axis == "grp":
            device, there = peer(axis, by)
            guarded(
                there,
                functools.partial(pl.semaphore_signal, barrier, inc=1, device_id=device, device_id_type=MESH),
            )
            greeted = greeted + there.astype(jnp.int32)

    loads = [
        pltpu.make_async_copy(source, target, load_sem.at[n])
        for n, (source, target) in enumerate(
            [(x_hbm, out_ref), (star_hbm, star_ref), (near_hbm, near_ref), (far_hbm, far_ref)]
        )
    ]
    for load in loads:
        load.start()

    def copy(step, slot):
        device, there = peer(*ways[slot])
        return (
            pltpu.make_async_remote_copy(
                src_ref=msg.at[slot],
                dst_ref=held.at[step, slot],
                send_sem=send_sem.at[step, slot],
                recv_sem=recv_sem.at[step, slot],
                device_id=device,
                device_id_type=MESH,
            ),
            there,
        )

    def start_slots(step, some):
        for slot in some:
            sent, there = copy(step, slot)
            guarded(there, sent.start)

    def wait_slots(step, some):
        for slot in some:
            sent, _ = copy(step, slot)
            axis, by = ways[slot]
            _, came = peer(axis, -by)
            guarded(came, sent.wait_recv)

    for slot in range(slots):
        axis, by = ways[slot]
        _, came = peer(axis, -by)
        if came is not None:

            @pl.when(jnp.logical_not(came))
            def _(slot=slot):
                for step in range(steps):
                    held[step, slot] = jnp.zeros(held.shape[2:], f32)

    width = 2 * LANES
    for pair in range(slots // 2):
        even, odd = ORDER[2 * pair], ORDER[2 * pair + 1]
        first, second = names_ref[even : even + 1, :], names_ref[odd : odd + 1, :]
        tile = slice(pair * LANES, (pair + 1) * LANES)
        straight = hot_of(0, elements, jnp.concatenate([first, second], 1))
        crossed = hot_of(0, elements, jnp.concatenate([second, first], 1))
        for again in range(2):
            hot_up[again * elements : (again + 1) * elements, tile] = straight
            hot_low[again * elements : (again + 1) * elements, tile] = crossed

    def paired(action):
        def one(i, carry):
            action(2 * i, 2)
            return carry

        lax.fori_loop(0, quantities // 2, one, 0)
        if quantities % 2:
            action(quantities - 1, 1)

    def split(q, count):
        field = jnp.concatenate([out_ref[q + n] for n in range(count)], 0)
        high, low = halves(field)
        at = pl.ds(pl.multiple_of(q * basis, 16) if not isinstance(q, int) else q * basis, count * basis)
        cat[at, :elements] = high
        cat[at, elements:] = low

    lane = lax.broadcasted_iota(jnp.int32, (upper, LANES), 1)

    def pack(number):
        lanes = slice(number * width, (number + 1) * width)
        up = dot(cat[:upper, :], hot_up[:, lanes])
        low = dot(cat[upper:rows, :], hot_low[:, lanes])
        for pair in range(width // LANES):
            tile = slice(pair * LANES, (pair + 1) * LANES)
            even, odd = ORDER[number * 4 + 2 * pair], ORDER[number * 4 + 2 * pair + 1]
            top, bottom = up[:, tile], low[:, tile]
            here = lane[:lower]
            msg[even, :lower, :] = jnp.where(here < half, top[:lower], bottom)
            msg[odd, :lower, :] = jnp.where(here < half, bottom, top[:lower])
            msg[even, lower:, :] = top[lower:]
            msg[odd, lower:, :] = top[lower:]

    def pack_and_send(step):
        pack(0)
        start_slots(step, NEAR)
        pack(1)
        start_slots(step, FAR)

    loads[0].wait()
    paired(split)
    pl.semaphore_wait(barrier, greeted)
    pack_and_send(0)

    for f in range(faces):
        names = faces_ref[f : f + 1, :]
        own = hot_of(0, elements, names)
        hot_own[f, :elements, :] = own
        hot_own[f, elements:, :] = own
        for g in range(2):
            for n in range(slots // 2):
                some = hot_of(elements + ORDER[g * (slots // 2) + n] * half, half, names)
                hot_halo[g * faces + f, n * half : (n + 1) * half, :] = some
                hot_halo[g * faces + f, group + n * half : group + (n + 1) * half, :] = some
    hot = hot_of(0, elements, recs_ref[0:1, :])
    hot_rec[:elements, :] = hot
    hot_rec[elements:, :] = hot
    lane_row = lax.broadcasted_iota(jnp.int32, (1, elements), 1)
    live = lane_row < count_ref[0]
    for load in loads[1:]:
        load.wait()

    def store_split(ref, f, q, count, parts, at, gap):
        high, low = halves(jnp.concatenate(parts, 0) if count > 1 else parts[0])
        where = pl.ds(pl.multiple_of(q * basis, 16) if not isinstance(q, int) else q * basis, count * basis)
        wide = high.shape[1]
        ref[f, where, pl.ds(at, wide)] = high
        ref[f, where, pl.ds(at + gap, wide)] = low

    def local_block(at, wide):
        def products(q, count):
            results = [dot(mats_ref[...], both[q + n, :, pl.ds(at, wide)]) for n in range(count)]
            for n in range(count):
                terms[q + n, :, :wide] = results[n][:own_rows]
            for f in range(faces):
                low = own_rows + f * basis
                store_split(tcat, f, q, count, [r[low : low + basis] for r in results], at, elements)

        paired(products)
        for sub in range(wide // LANES):
            lanes = pl.ds(at + sub * LANES, LANES)
            tile = slice(sub * LANES, (sub + 1) * LANES)
            for first, last in row_chunks(basis):

                def one_quantity(q, sums):
                    for n in range(dims + faces):
                        ref, k = (star_ref, n) if n < dims else (near_ref, n - dims)
                        term = terms[q, n * basis + first : n * basis + last, tile]
                        sums = sums + ref[:, q, k : k + 1, lanes] * term[None]
                    return sums

                start = jnp.zeros((quantities, last - first, LANES), f32)
                part[:, first:last, lanes] = lax.fori_loop(0, quantities, one_quantity, start)

    def own_face(f, carry):
        rterm[f] = dot(tcat[f], hot_own[f])
        return carry

    def halo_group(step, g):
        for pair in range(slots // 4):
            tile = slice(pair * LANES, (pair + 1) * LANES)
            at = g * (slots // 2) + 2 * pair
            even, odd = held[step, ORDER[at]], held[step, ORDER[at + 1]]
            hs[:upper, tile] = jnp.where(lane < half, even, odd)
            hs[upper:, tile] = pltpu.roll(jnp.where(lane < half, odd, even), half, 1)[: hs.shape[0] - upper]

        def products(q, count):
            results = []
            for n in range(count):
                start = (q + n) * basis
                start = start if isinstance(start, int) else pl.multiple_of(start, 8)
                results.append(dot(mats_ref[own_rows:, :], stacked_rows(hs[pl.ds(start, basis), :])))
            for f in range(faces):
                store_split(th, f, q, count, [r[f * basis : (f + 1) * basis] for r in results], 0, group)

        paired(products)

        def one_face(f, carry):
            rterm[f] = rterm[f] + dot(th[f], hot_halo[g * faces + f])
            return carry

        lax.fori_loop(0, faces, one_face, 0)

    def finish_block(number, carry):
        lanes = pl.ds(pl.multiple_of(number * LANES, LANES), LANES)
        alive = number * LANES + lax.broadcasted_iota(jnp.int32, (1, LANES), 1) < count_ref[0]
        for first, last in row_chunks(basis):

            def one_quantity(q, sums):
                for f in range(faces):
                    start = pl.multiple_of(q * basis + first, 8)
                    term = rterm[f, pl.ds(start, last - first), lanes]
                    sums = sums + far_ref[:, q, f : f + 1, lanes] * term[None]
                return sums

            sums = lax.fori_loop(0, quantities, one_quantity, part[:, first:last, lanes])
            field = out_ref[:, first:last, lanes]
            out_ref[:, first:last, lanes] = jnp.where(alive[None], field + sums, field)
        return carry

    def table_copy(step, by, source):
        return pltpu.make_async_remote_copy(
            src_ref=mine.at[step],
            dst_ref=tabs.at[step, source],
            send_sem=table_send.at[step, by],
            recv_sem=table_recv.at[step, source],
            device_id=dom_other(by),
            device_id_type=MESH,
        )

    def one_step(step, carry):
        for q in range(quantities):
            both[q] = stacked_rows(out_ref[q])
        at = 0
        while at < elements:
            wide = min(width, elements - at)
            local_block(at, wide)
            at += wide
        lax.fori_loop(0, faces, own_face, 0)
        wait_slots(step, NEAR)
        halo_group(step, 0)
        wait_slots(step, FAR)
        halo_group(step, 1)
        lax.fori_loop(0, elements // LANES, finish_block, 0)
        paired(split)
        for slot in range(slots):
            sent, there = copy(step, slot)
            guarded(there, sent.wait_send)

        @pl.when(step + 1 < steps)
        def _():
            pack_and_send(step + 1)

        total = jnp.zeros((1, elements), f32)
        picked = dot(cat[...], hot_rec[...])
        for q in range(quantities):
            field = out_ref[q]
            total = total + gains_ref[q : q + 1, :] * jnp.sum(field * field, axis=0, keepdims=True)
            here = picked[q * basis : (q + 1) * basis] * weight_ref[...]
            mine[step, q : q + 1, :] = jnp.sum(here, axis=0, keepdims=True)
        total = jnp.where(live, total, 0.0)
        folded = total[:, :LANES]
        for n in range(1, elements // LANES):
            folded = folded + total[:, n * LANES : (n + 1) * LANES]
        mine[step, quantities : quantities + 1, :] = folded
        mine[step, quantities + 1 : quantities + 2, :] = recs_ref[1:2, :].astype(f32)

        def start(by, carry):
            table_copy(step, by, me).start()
            return carry

        lax.fori_loop(1, size, start, 0)
        tabs[step, me] = mine[step]
        return carry

    unused = mine.shape[1] - quantities - 2
    for step in range(steps):
        mine[step, quantities + 2 :, :] = jnp.zeros((unused, LANES), f32)
    lax.fori_loop(0, steps, one_step, 0)

    for step in range(steps):

        def finish(by, carry):
            table_copy(step, by, me).wait_send()
            table_copy(step, by, lax.rem(me + by, size)).wait_recv()
            return carry

        lax.fori_loop(1, size, finish, 0)
    wanted = (me * receivers + lax.broadcasted_iota(jnp.int32, (receivers, LANES), 0)).astype(f32)
    hits, values = [], []
    for source in range(size):
        slot_row = tabs[0, source, quantities + 1 : quantities + 2, :]
        hits.append(jnp.where(wanted == slot_row, 1.0, 0.0).astype(bf16))
        values.append(jnp.concatenate([tabs[step, source] for step in range(steps)], 0))
    hit = jnp.concatenate(hits, 1)
    value = jnp.concatenate(values, 1)
    contract = (((1,), (1,)), ((), ()))
    result = 0.0
    for piece in halves(value):
        result = result + lax.dot_general(piece, hit, contract, preferred_element_type=f32)
    deep = mine.shape[1]
    denominator = float(size * elements * basis * quantities)
    for step in range(steps):
        for q in range(quantities):
            trace_ref[q, step : step + 1, :] = result[step * deep + q : step * deep + q + 1, :]
        row = tabs[step, 0, quantities : quantities + 1, :]
        for source in range(1, size):
            row = row + tabs[step, source, quantities : quantities + 1, :]
        energy_ref[0:1, step : step + 1] = jnp.sum(row, axis=1, keepdims=True) * (0.5 / denominator)


def per_device(
    element_state,
    stiffness,
    flux_local,
    flux_remote,
    star_matrix,
    face_local,
    face_remote,
    energy_weight,
    face_neighbour,
    element_count,
    send_count,
    send_element,
    receiver_element,
    receiver_slot,
    receiver_weight,
):
    basis, quantities, elements = element_state.shape
    slots, capacity = send_element.shape[1:]
    receivers = receiver_slot.shape[0]
    dimensions, faces = stiffness.shape[0], flux_local.shape[0]
    size = lax.axis_size("dom")
    rows = quantities * basis
    upper = (rows // 2 + 15) // 16 * 16
    group = slots // 2 * capacity
    deep = (quantities + 2 + 7) // 8 * 8

    mats = stacked_matrix(jnp.concatenate([stiffness, -flux_local, -flux_remote], 0))
    mats = mats.reshape(-1, mats.shape[2])
    slot_live = jnp.arange(capacity)[None, :] < send_count[0][:, None]
    names = jnp.where(slot_live, send_element[0], -1)
    recs = jnp.pad(
        jnp.stack([receiver_element, receiver_slot]), ((0, 0), (0, LANES - receivers)), constant_values=-1
    )
    rec_weight = jnp.pad(receiver_weight, ((0, 0), (0, LANES - receivers)))
    fields = jnp.transpose(element_state, (1, 0, 2))
    stars = jnp.transpose(star_matrix, (1, 2, 0, 3))
    near = jnp.transpose(face_local, (1, 2, 0, 3))
    far = jnp.transpose(face_remote, (1, 2, 0, 3))

    in_vmem = pl.BlockSpec(memory_space=pltpu.VMEM)
    in_hbm = pl.BlockSpec(memory_space=pltpu.HBM)
    in_smem = pl.BlockSpec(memory_space=pltpu.SMEM)
    vmem = pltpu.VMEM
    state, energy, traces = pl.pallas_call(
        steps_kernel,
        out_shape=(
            jax.ShapeDtypeStruct((quantities, basis, elements), f32),
            jax.ShapeDtypeStruct((1, TIME_STEPS), f32),
            jax.ShapeDtypeStruct((quantities, TIME_STEPS, receivers), f32),
        ),
        in_specs=[in_hbm] * 4 + [in_vmem] * 6 + [in_smem],
        out_specs=(in_vmem,) * 3,
        scratch_shapes=[
            vmem(stars.shape, f32),
            vmem(near.shape, f32),
            vmem(far.shape, f32),
            vmem((quantities, 4 * basis, elements), bf16),
            vmem((rows, 2 * elements), bf16),
            vmem((quantities, (dimensions + faces) * basis, 2 * LANES), f32),
            vmem((quantities, basis, elements), f32),
            vmem((faces, rows, 2 * elements), bf16),
            vmem((faces, rows, elements), f32),
            vmem((rows, group), f32),
            vmem((faces, rows, 2 * group), bf16),
            vmem((faces, 2 * elements, elements), bf16),
            vmem((2 * faces, 2 * group, elements), bf16),
            vmem((2 * elements, slots * capacity), bf16),
            vmem((2 * elements, slots * capacity), bf16),
            vmem((2 * elements, LANES), bf16),
            vmem((slots, upper, LANES), f32),
            vmem((TIME_STEPS, slots, upper, LANES), f32),
            vmem((TIME_STEPS, deep, LANES), f32),
            vmem((TIME_STEPS, size, deep, LANES), f32),
            pltpu.SemaphoreType.DMA((4,)),
            pltpu.SemaphoreType.DMA((TIME_STEPS, slots)),
            pltpu.SemaphoreType.DMA((TIME_STEPS, slots)),
            pltpu.SemaphoreType.DMA((TIME_STEPS, size)),
            pltpu.SemaphoreType.DMA((TIME_STEPS, size)),
        ],
        compiler_params=pltpu.CompilerParams(
            vmem_limit_bytes=60 << 20, collective_id=0, has_side_effects=True
        ),
        name="steps",
    )(
        fields, stars, near, far,
        mats, rec_weight, face_neighbour, names, energy_weight, recs, element_count,
    )
    return (
        jnp.transpose(state, (1, 0, 2)),
        energy,
        jnp.transpose(traces, (1, 0, 2)),
    )


def solution(mesh):
    both = ("grp", "dom")
    return jax.shard_map(
        per_device,
        mesh=mesh,
        in_specs=(
            P(None, None, both),
            P(),
            P(),
            P(),
            P(None, None, None, both),
            P(None, None, None, both),
            P(None, None, None, both),
            P(None, both),
            P(None, both),
            P(both),
            P(both, None),
            P(both, None, None),
            P(both),
            P(both),
            P(None, both),
        ),
        out_specs=(P(None, None, both), P("grp", None), P(None, None, both)),
        check_vma=False,
    )
```

time: 164 us -> 118 us (0.72)
  Pallas kernels: 150 us -> 105 us
  local copies, waits for them, and re-layouts: 7.84 us -> 5.54 us
  other arithmetic: 3.58 us -> 5.86 us
    pallas_call x11 -> x1, Pallas kernels: 150 us -> 105 us  [per_device(): pl.pallas_call(steps_kernel, out_shape=(jax.ShapeDtypeStruct((quantities,...]
    neg x1 -> x2, other arithmetic: 0.01 us -> 1.82 us  [the longest x1 0.91 us: per_device(): -flux_remote]
    unnamed x22 -> x8, local copies, waits for them, and re-layouts: 4.86 us -> 4.35 us
where the time goes in v1:
time: 118 us
  Pallas kernels  105 us (89%)
  other arithmetic  5.86 us (5%)
  local copies, waits for them, and re-layouts  5.54 us (5%)
  between operations  1.32 us (1%)
    pallas_call x1, Pallas kernels, per_device(): pl.pallas_call(steps_kernel, out_shape=(jax.ShapeDtypeStruct((quantities,...  105 us
    unnamed x8, local copies, waits for them, and re-layouts  4.35 us

profile of v1, /device:TPU:0, one launch (start us, length us, event | category | flops | bytes accessed | tf_op | source)
XLA Modules:
  0.0 117.9 jit_solution(16150859385140058358)
XLA Ops:
  1.3 0.7 pad_add_fusion
  2.0 0.6 pad.9.recs_ref
  2.5 1.4 %bitcast_select_fusion.names_ref = s32[8,64]{1,0:T(8,128)} fusion(s32[1,8,64]{2,1,0:T(8,128)} %param.26, s32[8]{0:T(128)} %bitcast.20), kind=kLoop, calls=%fused_computation.5 | loop fusion | flops 1024 | bytes 4128 | tf_op jit(solution)/shard_map/jit(_where)/select_n | solution.py:436
  3.9 0.8 copy.18
  4.7 0.6 pad.8.weight_ref
  5.3 0.9 neg.6
  6.2 0.9 neg.7
  7.1 0.9 pad_maximum_fusion
  8.0 0.1 reduce-precision_convert_fusion
  8.1 1.0 pad_maximum_fusion.1.mats_ref
  9.1 105.2 %steps.1 = (f32[9,56,640]{2,1,0:T(8,128)}, f32[1,3]{1,0:T(1,128)}, f32[9,3,16]{2,1,0:T(4,128)}) custom-call(f32[9,56,640]{2,1,0:T(8,128)} %bitcast.14, f32[9,9,3,640]{3,2,1,0:T(4,128)} %bitcast.16, f32[9,9,4,640]{3,2,1,0:T(4,128)} %bitcast.17, f32[9,9,4,640]{3,2,1,0:T(4,128)} %bitcast.18, bf16[616,224]{1,0:T(8,128)(2,1)} %pad_maximum_fusion.1.mats_ref, ...), custom_call_target="tpu_custom_call" | custom-call | tf_op jit(solution)/shard_map/steps/pallas_call | solution.py:450
  114.3 0.0 copy-start.1
  114.3 0.0 copy-start
  114.3 2.4 %copy.23 = f32[56,9,640]{2,0,1:T(8,128)} copy(f32[56,9,640]{2,0,1:T(8,128)} %bitcast.15) | data formatting | bytes 2580480
  116.8 0.0 copy-done.1
  116.8 0.5 copy.24
  117.3 0.0 copy-done
  117.3 0.6 copy.25
Async XLA Ops:
  114.3 2.5 %copy-start.1 = (f32[1,3]{1,0:T(1,128)S(1)}, f32[1,3]{1,0:T(1,128)}, u32[]{:S(2)}) copy-start(f32[1,3]{1,0:T(1,128)} %get-tuple-element.15) | copy-start | bytes 40
  114.3 3.0 %copy-start = (f32[9,3,16]{2,1,0:T(4,128)S(1)}, f32[9,3,16]{2,1,0:T(4,128)}, u32[]{:S(2)}) copy-start(f32[9,3,16]{2,1,0:T(4,128)} %get-tuple-element.8) | copy-start | bytes 5188

commit v2 on v1

--- a/solution.py
+++ b/solution.py
@@ -13,6 +13,7 @@
 NEAR = (0, PEER_REACH, 2 * PEER_REACH, 2 * PEER_REACH + 1)
 FAR = tuple(s for n in range(1, PEER_REACH) for s in (n, PEER_REACH + n))
 ORDER = NEAR + FAR
+GROUPS = ((0, 4), (4, 4))
 MESH = pl.DeviceIdType.MESH
 f32, bf16 = jnp.float32, jnp.bfloat16
 
@@ -30,13 +31,6 @@
     high = field.astype(bf16).astype(f32)
     both = jnp.concatenate([high, field - high], 0).astype(bf16)
     return jnp.concatenate([both, both], 0)
-
-
-def stacked_matrix(matrices):
-    high = lax.reduce_precision(matrices, 8, 7)
-    low = (matrices - high).astype(bf16)
-    high = high.astype(bf16)
-    return jnp.concatenate([high, high, low, low], 2)
 
 
 def row_chunks(rows):
@@ -74,11 +68,13 @@
 
 
 def steps_kernel(
-    x_hbm, star_hbm, near_hbm, far_hbm,
-    mats_ref, weight_ref, faces_ref, names_ref, gains_ref, recs_ref, count_ref,
+    names_hbm, x_hbm, faces_hbm, stiff_hbm, own_hbm, other_hbm, star_hbm, near_hbm, far_hbm,
+    gains_hbm, element_hbm, slot_hbm, weight_hbm, count_ref, sent_ref,
     out_ref, energy_ref, trace_ref,
-    star_ref, near_ref, far_ref, both, cat, terms, part, tcat, rterm, hs, th,
-    hot_own, hot_halo, hot_up, hot_low, hot_rec, msg, held, mine, tabs,
+    names_ref, faces_ref, stiff_ref, own_ref, other_ref, star_ref, near_ref, far_ref,
+    gains_ref, element_ref, slot_ref, weight_ref,
+    mats_ref, both, cat, terms, part, tcat, rterm, hs, th,
+    hot_own, hot_halo, hot_up, hot_low, hot_rec, wide_weight, msg, held, mine, tabs,
     load_sem, send_sem, recv_sem, table_send, table_recv,
 ):
     quantities, basis, elements = out_ref.shape
@@ -90,12 +86,34 @@
     faces = far_ref.shape[2]
     dims = star_ref.shape[2]
     own_rows = (dims + faces) * basis
-    group = slots // 2 * half
     steps = TIME_STEPS
     size = lax.axis_size("dom")
     me = lax.axis_index("dom")
     receivers = trace_ref.shape[2]
     ways = [halo_ways(slot) for slot in range(slots)]
+
+    loads = [
+        pltpu.make_async_copy(source, target, load_sem.at[n])
+        for n, (source, target) in enumerate(
+            [
+                (names_hbm, names_ref),
+                (x_hbm, out_ref),
+                (faces_hbm, faces_ref),
+                (stiff_hbm, stiff_ref),
+                (own_hbm, own_ref),
+                (other_hbm, other_ref),
+                (star_hbm, star_ref),
+                (near_hbm, near_ref),
+                (far_hbm, far_ref),
+                (gains_hbm, gains_ref),
+                (element_hbm, element_ref),
+                (slot_hbm, slot_ref),
+                (weight_hbm, weight_ref),
+            ]
+        )
+    ]
+    for load in loads:
+        load.start()
 
     barrier = pltpu.get_barrier_semaphore()
 
@@ -116,15 +134,6 @@
                 functools.partial(pl.semaphore_signal, barrier, inc=1, device_id=device, device_id_type=MESH),
             )
             greeted = greeted + there.astype(jnp.int32)
-
-    loads = [
-        pltpu.make_async_copy(source, target, load_sem.at[n])
-        for n, (source, target) in enumerate(
-            [(x_hbm, out_ref), (star_hbm, star_ref), (near_hbm, near_ref), (far_hbm, far_ref)]
-        )
-    ]
-    for load in loads:
-        load.start()
 
     def copy(step, slot):
         device, there = peer(*ways[slot])
@@ -163,9 +172,13 @@
                     held[step, slot] = jnp.zeros(held.shape[2:], f32)
 
     width = 2 * LANES
+    loads[0].wait()
     for pair in range(slots // 2):
         even, odd = ORDER[2 * pair], ORDER[2 * pair + 1]
-        first, second = names_ref[even : even + 1, :], names_ref[odd : odd + 1, :]
+        place = lax.broadcasted_iota(jnp.int32, (1, half), 1)
+        first, second = (
+            jnp.where(place < sent_ref[0, o], names_ref[o : o + 1, :], -1) for o in (even, odd)
+        )
         tile = slice(pair * LANES, (pair + 1) * LANES)
         straight = hot_of(0, elements, jnp.concatenate([first, second], 1))
         crossed = hot_of(0, elements, jnp.concatenate([second, first], 1))
@@ -211,28 +224,42 @@
         pack(1)
         start_slots(step, FAR)
 
-    loads[0].wait()
+    loads[1].wait()
     paired(split)
     pl.semaphore_wait(barrier, greeted)
     pack_and_send(0)
+
+    for load in loads[2:]:
+        load.wait()
+    sources = [(stiff_ref, n, 1.0) for n in range(dims)]
+    sources += [(ref, n, -1.0) for ref in (own_ref, other_ref) for n in range(faces)]
+    for n in range(0, len(sources), 2):
+        some = jnp.concatenate([ref[k] * sign for ref, k, sign in sources[n : n + 2]], 0)
+        high = some.astype(bf16).astype(f32)
+        low = some - high
+        mats_ref[n * basis : n * basis + some.shape[0], :] = jnp.concatenate([high, high, low, low], 1).astype(bf16)
 
     for f in range(faces):
         names = faces_ref[f : f + 1, :]
         own = hot_of(0, elements, names)
         hot_own[f, :elements, :] = own
         hot_own[f, elements:, :] = own
-        for g in range(2):
-            for n in range(slots // 2):
-                some = hot_of(elements + ORDER[g * (slots // 2) + n] * half, half, names)
-                hot_halo[g * faces + f, n * half : (n + 1) * half, :] = some
-                hot_halo[g * faces + f, group + n * half : group + (n + 1) * half, :] = some
-    hot = hot_of(0, elements, recs_ref[0:1, :])
+        for begin, many in GROUPS:
+            for n in range(many):
+                some = hot_of(elements + ORDER[begin + n] * half, half, names)
+                at = (2 * begin + n) * half
+                hot_halo[f, at : at + half, :] = some
+                hot_halo[f, at + many * half : at + (many + 1) * half, :] = some
+    absent = jnp.full((1, LANES - receivers), -1, jnp.int32)
+    hot = hot_of(0, elements, jnp.concatenate([element_ref[...], absent], 1))
+    slot_row = jnp.concatenate([slot_ref[...], absent], 1).astype(f32)
+    wide_weight[...] = jnp.concatenate(
+        [weight_ref[...].T, jnp.zeros((basis, LANES - receivers), f32)], 1
+    )
     hot_rec[:elements, :] = hot
     hot_rec[elements:, :] = hot
     lane_row = lax.broadcasted_iota(jnp.int32, (1, elements), 1)
     live = lane_row < count_ref[0]
-    for load in loads[1:]:
-        load.wait()
 
     def store_split(ref, f, q, count, parts, at, gap):
         high, low = halves(jnp.concatenate(parts, 0) if count > 1 else parts[0])
@@ -245,35 +272,55 @@
         def products(q, count):
             results = [dot(mats_ref[...], both[q + n, :, pl.ds(at, wide)]) for n in range(count)]
             for n in range(count):
-                terms[q + n, :, :wide] = results[n][:own_rows]
+                terms[q + n, :, pl.ds(at, wide)] = results[n][:own_rows]
             for f in range(faces):
                 low = own_rows + f * basis
                 store_split(tcat, f, q, count, [r[low : low + basis] for r in results], at, elements)
 
         paired(products)
-        for sub in range(wide // LANES):
-            lanes = pl.ds(at + sub * LANES, LANES)
-            tile = slice(sub * LANES, (sub + 1) * LANES)
-            for first, last in row_chunks(basis):
-
-                def one_quantity(q, sums):
-                    for n in range(dims + faces):
-                        ref, k = (star_ref, n) if n < dims else (near_ref, n - dims)
-                        term = terms[q, n * basis + first : n * basis + last, tile]
-                        sums = sums + ref[:, q, k : k + 1, lanes] * term[None]
-                    return sums
-
-                start = jnp.zeros((quantities, last - first, LANES), f32)
-                part[:, first:last, lanes] = lax.fori_loop(0, quantities, one_quantity, start)
-
-    def own_face(f, carry):
-        rterm[f] = dot(tcat[f], hot_own[f])
-        return carry
-
-    def halo_group(step, g):
-        for pair in range(slots // 4):
+
+    def window_part(at, wide):
+        def gather(f):
+            lanes = pl.ds(at, wide)
+            picked = dot(tcat[f], hot_own[f, :, lanes])
+            rterm[f, :, :, lanes] = picked.reshape(quantities, basis, wide)
+
+        def local(lanes, first, last):
+            sums = [jnp.zeros((last - first, LANES), f32) for _ in range(quantities)]
+            for q in range(quantities):
+                for n in range(dims + faces):
+                    ref, k = (star_ref, n) if n < dims else (near_ref, n - dims)
+                    term = terms[q, n * basis + first : n * basis + last, lanes]
+                    for p in range(quantities):
+                        sums[p] = sums[p] + ref[p, q, k : k + 1, lanes] * term
+            for p in range(quantities):
+                part[p, first:last, lanes] = sums[p]
+
+        work = [
+            functools.partial(local, pl.ds(at + sub * LANES, LANES), first, last)
+            for sub in range(wide // LANES)
+            for first, last in row_chunks(basis)
+        ]
+        for n in range(max(len(work), faces)):
+            if n < faces:
+                gather(n)
+            if n < len(work):
+                work[n]()
+
+    def in_parts(action):
+        def one(number, carry):
+            action(pl.multiple_of(number * width, width), width)
+            return carry
+
+        lax.fori_loop(0, elements // width, one, 0)
+        if elements % width:
+            action(elements - elements % width, elements % width)
+
+    def halo_terms(step, begin, many):
+        cols = many * half
+        for pair in range(many // 2):
             tile = slice(pair * LANES, (pair + 1) * LANES)
-            at = g * (slots // 2) + 2 * pair
+            at = begin + 2 * pair
             even, odd = held[step, ORDER[at]], held[step, ORDER[at + 1]]
             hs[:upper, tile] = jnp.where(lane < half, even, odd)
             hs[upper:, tile] = pltpu.roll(jnp.where(lane < half, odd, even), half, 1)[: hs.shape[0] - upper]
@@ -283,34 +330,42 @@
             for n in range(count):
                 start = (q + n) * basis
                 start = start if isinstance(start, int) else pl.multiple_of(start, 8)
-                results.append(dot(mats_ref[own_rows:, :], stacked_rows(hs[pl.ds(start, basis), :])))
+                results.append(dot(mats_ref[own_rows:, :], stacked_rows(hs[pl.ds(start, basis), :cols])))
             for f in range(faces):
-                store_split(th, f, q, count, [r[f * basis : (f + 1) * basis] for r in results], 0, group)
+                store_split(th, f, q, count, [r[f * basis : (f + 1) * basis] for r in results], 0, cols)
 
         paired(products)
 
+    def add_halo(f, begin, many, lanes, wide):
+        cols = many * half
+        late = dot(th[f, :, : 2 * cols], hot_halo[f, 2 * begin * half : 2 * (begin + many) * half, lanes])
+        rterm[f, :, :, lanes] = rterm[f, :, :, lanes] + late.reshape(quantities, basis, wide)
+
+    def halo_group(step, begin, many):
+        halo_terms(step, begin, many)
+
         def one_face(f, carry):
-            rterm[f] = rterm[f] + dot(th[f], hot_halo[g * faces + f])
+            add_halo(f, begin, many, slice(None), elements)
             return carry
 
         lax.fori_loop(0, faces, one_face, 0)
 
-    def finish_block(number, carry):
-        lanes = pl.ds(pl.multiple_of(number * LANES, LANES), LANES)
-        alive = number * LANES + lax.broadcasted_iota(jnp.int32, (1, LANES), 1) < count_ref[0]
-        for first, last in row_chunks(basis):
-
-            def one_quantity(q, sums):
+    def finish_part(at, wide):
+        for f in range(faces):
+            add_halo(f, *GROUPS[-1], pl.ds(at, wide), wide)
+        for sub in range(wide // LANES):
+            lanes = pl.ds(at + sub * LANES, LANES)
+            alive = at + sub * LANES + lax.broadcasted_iota(jnp.int32, (1, LANES), 1) < count_ref[0]
+            for first, last in row_chunks(basis):
+                sums = [part[p, first:last, lanes] for p in range(quantities)]
                 for f in range(faces):
-                    start = pl.multiple_of(q * basis + first, 8)
-                    term = rterm[f, pl.ds(start, last - first), lanes]
-                    sums = sums + far_ref[:, q, f : f + 1, lanes] * term[None]
-                return sums
-
-            sums = lax.fori_loop(0, quantities, one_quantity, part[:, first:last, lanes])
-            field = out_ref[:, first:last, lanes]
-            out_ref[:, first:last, lanes] = jnp.where(alive[None], field + sums, field)
-        return carry
+                    for q in range(quantities):
+                        term = rterm[f, q, first:last, lanes]
+                        for p in range(quantities):
+                            sums[p] = sums[p] + far_ref[p, q, f : f + 1, lanes] * term
+                for p in range(quantities):
+                    field = out_ref[p, first:last, lanes]
+                    out_ref[p, first:last, lanes] = jnp.where(alive, field + sums[p], field)
 
     def table_copy(step, by, source):
         return pltpu.make_async_remote_copy(
@@ -330,12 +385,14 @@
             wide = min(width, elements - at)
             local_block(at, wide)
             at += wide
-        lax.fori_loop(0, faces, own_face, 0)
-        wait_slots(step, NEAR)
-        halo_group(step, 0)
-        wait_slots(step, FAR)
-        halo_group(step, 1)
-        lax.fori_loop(0, elements // LANES, finish_block, 0)
+        in_parts(window_part)
+        for begin, many in GROUPS:
+            wait_slots(step, ORDER[begin : begin + many])
+            if begin + many < slots:
+                halo_group(step, begin, many)
+            else:
+                halo_terms(step, begin, many)
+        in_parts(finish_part)
         paired(split)
         for slot in range(slots):
             sent, there = copy(step, slot)
@@ -350,14 +407,14 @@
         for q in range(quantities):
             field = out_ref[q]
             total = total + gains_ref[q : q + 1, :] * jnp.sum(field * field, axis=0, keepdims=True)
-            here = picked[q * basis : (q + 1) * basis] * weight_ref[...]
+            here = picked[q * basis : (q + 1) * basis] * wide_weight[...]
             mine[step, q : q + 1, :] = jnp.sum(here, axis=0, keepdims=True)
         total = jnp.where(live, total, 0.0)
         folded = total[:, :LANES]
         for n in range(1, elements // LANES):
             folded = folded + total[:, n * LANES : (n + 1) * LANES]
         mine[step, quantities : quantities + 1, :] = folded
-        mine[step, quantities + 1 : quantities + 2, :] = recs_ref[1:2, :].astype(f32)
+        mine[step, quantities + 1 : quantities + 2, :] = slot_row
 
         def start(by, carry):
             table_copy(step, by, me).start()
@@ -383,8 +440,8 @@
     wanted = (me * receivers + lax.broadcasted_iota(jnp.int32, (receivers, LANES), 0)).astype(f32)
     hits, values = [], []
     for source in range(size):
-        slot_row = tabs[0, source, quantities + 1 : quantities + 2, :]
-        hits.append(jnp.where(wanted == slot_row, 1.0, 0.0).astype(bf16))
+        place_row = tabs[0, source, quantities + 1 : quantities + 2, :]
+        hits.append(jnp.where(wanted == place_row, 1.0, 0.0).astype(bf16))
         values.append(jnp.concatenate([tabs[step, source] for step in range(steps)], 0))
     hit = jnp.concatenate(hits, 1)
     value = jnp.concatenate(values, 1)
@@ -401,6 +458,20 @@
         for source in range(1, size):
             row = row + tabs[step, source, quantities : quantities + 1, :]
         energy_ref[0:1, step : step + 1] = jnp.sum(row, axis=1, keepdims=True) * (0.5 / denominator)
+
+
+def store_kernel(state_hbm, trace_hbm, energy_hbm, out_hbm, trace_out, energy_out, held, trace, energy, load_sem, store_sem):
+    ways = [(state_hbm.at[n], held.at[n], out_hbm.at[n]) for n in range(held.shape[0])]
+    ways += [(trace_hbm, trace, trace_out), (energy_hbm, energy, energy_out)]
+    loads = [pltpu.make_async_copy(a, b, load_sem.at[n]) for n, (a, b, _) in enumerate(ways)]
+    stores = [pltpu.make_async_copy(b, c, store_sem.at[n]) for n, (_, b, c) in enumerate(ways)]
+    for load in loads:
+        load.start()
+    for load, store in zip(loads, stores):
+        load.wait()
+        store.start()
+    for store in stores:
+        store.wait()
 
 
 def per_device(
@@ -430,19 +501,26 @@
     group = slots // 2 * capacity
     deep = (quantities + 2 + 7) // 8 * 8
 
-    mats = stacked_matrix(jnp.concatenate([stiffness, -flux_local, -flux_remote], 0))
-    mats = mats.reshape(-1, mats.shape[2])
-    slot_live = jnp.arange(capacity)[None, :] < send_count[0][:, None]
-    names = jnp.where(slot_live, send_element[0], -1)
-    recs = jnp.pad(
-        jnp.stack([receiver_element, receiver_slot]), ((0, 0), (0, LANES - receivers)), constant_values=-1
-    )
-    rec_weight = jnp.pad(receiver_weight, ((0, 0), (0, LANES - receivers)))
     fields = jnp.transpose(element_state, (1, 0, 2))
     stars = jnp.transpose(star_matrix, (1, 2, 0, 3))
     near = jnp.transpose(face_local, (1, 2, 0, 3))
     far = jnp.transpose(face_remote, (1, 2, 0, 3))
 
+    arrays = (
+        send_element[0],
+        fields,
+        face_neighbour,
+        stiffness,
+        flux_local,
+        flux_remote,
+        stars,
+        near,
+        far,
+        energy_weight,
+        receiver_element[None, :],
+        receiver_slot[None, :],
+        receiver_weight.T,
+    )
     in_vmem = pl.BlockSpec(memory_space=pltpu.VMEM)
     in_hbm = pl.BlockSpec(memory_space=pltpu.HBM)
     in_smem = pl.BlockSpec(memory_space=pltpu.SMEM)
@@ -454,43 +532,52 @@
             jax.ShapeDtypeStruct((1, TIME_STEPS), f32),
             jax.ShapeDtypeStruct((quantities, TIME_STEPS, receivers), f32),
         ),
-        in_specs=[in_hbm] * 4 + [in_vmem] * 6 + [in_smem],
+        in_specs=[in_hbm] * len(arrays) + [in_smem] * 2,
         out_specs=(in_vmem,) * 3,
         scratch_shapes=[
-            vmem(stars.shape, f32),
-            vmem(near.shape, f32),
-            vmem(far.shape, f32),
+            *[vmem(a.shape, a.dtype) for n, a in enumerate(arrays) if n != 1],
+            vmem(((dimensions + 2 * faces) * basis, 4 * basis), bf16),
             vmem((quantities, 4 * basis, elements), bf16),
             vmem((rows, 2 * elements), bf16),
-            vmem((quantities, (dimensions + faces) * basis, 2 * LANES), f32),
+            vmem((quantities, (dimensions + faces) * basis, elements), f32),
             vmem((quantities, basis, elements), f32),
             vmem((faces, rows, 2 * elements), bf16),
-            vmem((faces, rows, elements), f32),
+            vmem((faces, quantities, basis, elements), f32),
             vmem((rows, group), f32),
             vmem((faces, rows, 2 * group), bf16),
             vmem((faces, 2 * elements, elements), bf16),
-            vmem((2 * faces, 2 * group, elements), bf16),
+            vmem((faces, 2 * slots * capacity, elements), bf16),
             vmem((2 * elements, slots * capacity), bf16),
             vmem((2 * elements, slots * capacity), bf16),
             vmem((2 * elements, LANES), bf16),
+            vmem((basis, LANES), f32),
             vmem((slots, upper, LANES), f32),
             vmem((TIME_STEPS, slots, upper, LANES), f32),
             vmem((TIME_STEPS, deep, LANES), f32),
             vmem((TIME_STEPS, size, deep, LANES), f32),
-            pltpu.SemaphoreType.DMA((4,)),
+            pltpu.SemaphoreType.DMA((len(arrays),)),
             pltpu.SemaphoreType.DMA((TIME_STEPS, slots)),
             pltpu.SemaphoreType.DMA((TIME_STEPS, slots)),
             pltpu.SemaphoreType.DMA((TIME_STEPS, size)),
             pltpu.SemaphoreType.DMA((TIME_STEPS, size)),
         ],
         compiler_params=pltpu.CompilerParams(
-            vmem_limit_bytes=60 << 20, collective_id=0, has_side_effects=True
+            vmem_limit_bytes=56 << 20, collective_id=0, has_side_effects=True
         ),
         name="steps",
-    )(
-        fields, stars, near, far,
-        mats, rec_weight, face_neighbour, names, energy_weight, recs, element_count,
-    )
+    )(*arrays, element_count, send_count)
+    state, traces, energy = pl.pallas_call(
+        store_kernel,
+        out_shape=tuple(jax.ShapeDtypeStruct(a.shape, f32) for a in (state, traces, energy)),
+        in_specs=[in_hbm] * 3,
+        out_specs=(in_hbm,) * 3,
+        scratch_shapes=[
+            *[vmem(a.shape, f32) for a in (state, traces, energy)],
+            pltpu.SemaphoreType.DMA((quantities + 2,)),
+            pltpu.SemaphoreType.DMA((quantities + 2,)),
+        ],
+        name="store",
+    )(state, traces, energy)
     return (
         jnp.transpose(state, (1, 0, 2)),
         energy,

time: 118 us -> 100 us (0.85)
  Pallas kernels: 105 us -> 98.4 us
  other arithmetic: 5.86 us -> 0 us
  local copies, waits for them, and re-layouts: 5.54 us -> 0 us
    pallas_call x1, Pallas kernels: 105 us -> 96.1 us  [per_device(): pl.pallas_call(steps_kernel, out_shape=(jax.ShapeDtypeStruct((quantities,...]
    unnamed x8 -> x0, local copies, waits for them, and re-layouts: 4.35 us -> none
    pallas_call x0 -> x1, Pallas kernels: none -> 2.24 us  [per_device(): pl.pallas_call(store_kernel, out_shape=tuple((jax.ShapeDtypeStruct(a.shap...]
    concatenate x2 -> x0, other arithmetic: 1.96 us -> none  [the longest x1 1.04 us: stacked_matrix(): return jnp.concatenate([high, high, low, low], 2)]
    neg x2 -> x0, other arithmetic: 1.82 us -> none  [the longest x1 0.91 us: per_device(): -flux_remote]
    select_n x1 -> x0, other arithmetic: 1.35 us -> none  [per_device(): names = jnp.where(slot_live, send_element[0], -1)]
    pad x2 -> x0, local copies, waits for them, and re-layouts: 1.2 us -> none  [the longest x1 0.62 us: per_device(): rec_weight = jnp.pad(receiver_weight, ((0, 0), (0, LANES - receivers)))]
where the time goes in v2:
time: 100 us; the launch traced here: 99.8 us
  Pallas kernels  98.4 us (98%)
  between operations  1.45 us (1%)
    pallas_call x1, Pallas kernels, per_device(): pl.pallas_call(steps_kernel, out_shape=(jax.ShapeDtypeStruct((quantities,...  96.1 us
    pallas_call x1, Pallas kernels, per_device(): pl.pallas_call(store_kernel, out_shape=tuple((jax.ShapeDtypeStruct(a.shap...  2.24 us

profile of v2, /device:TPU:0, one launch (start us, length us, event | category | flops | bytes accessed | tf_op | source)
XLA Modules:
  0.0 99.8 jit_solution(10545985899146349851)
XLA Ops:
  1.3 96.1 %steps.1 = (f32[9,56,640]{2,1,0:T(8,128)}, f32[1,3]{1,0:T(1,128)}, f32[9,3,16]{2,1,0:T(4,128)}) custom-call(s32[8,64]{1,0:T(8,128)} %bitcast.15, f32[9,56,640]{2,1,0:T(8,128)} %bitcast.10, s32[4,640]{1,0:T(4,128)} %faces_hbm.1, f32[3,56,56]{2,1,0:T(8,128)} %stiff_hbm.1, f32[4,56,56]{2,1,0:T(8,128)} %own_hbm.1, f32[4,56,56]{2,1,0:T(8,128)} %other_hbm.1, ...), custom_call_target="tpu_custom_call" | custom-call | tf_op jit(solution)/shard_map/steps/pallas_call | solution.py:528
  97.4 2.2 %store.1 = (f32[9,56,640]{2,1,0:T(8,128)}, f32[9,3,16]{2,1,0:T(4,128)}, f32[1,3]{1,0:T(1,128)}) custom-call(f32[9,56,640]{2,1,0:T(8,128)} %get-tuple-element.9.state_hbm, f32[9,3,16]{2,1,0:T(4,128)} %get-tuple-element.10.trace_hbm, f32[1,3]{1,0:T(1,128)} %get-tuple-element.11.energy_hbm), custom_call_target="tpu_custom_call" | custom-call | tf_op jit(solution)/shard_map/store/pallas_call | solution.py:569

commit v3 on v2

--- a/solution.py
+++ b/solution.py
@@ -102,17 +102,17 @@
                 (stiff_hbm, stiff_ref),
                 (own_hbm, own_ref),
                 (other_hbm, other_ref),
-                (star_hbm, star_ref),
-                (near_hbm, near_ref),
-                (far_hbm, far_ref),
                 (gains_hbm, gains_ref),
                 (element_hbm, element_ref),
                 (slot_hbm, slot_ref),
                 (weight_hbm, weight_ref),
+                (star_hbm, star_ref),
+                (near_hbm, near_ref),
+                (far_hbm, far_ref),
             ]
         )
     ]
-    for load in loads:
+    for load in loads[:-3]:
         load.start()
 
     barrier = pltpu.get_barrier_semaphore()
@@ -225,21 +225,14 @@
         start_slots(step, FAR)
 
     loads[1].wait()
+    for load in loads[-3:]:
+        load.start()
     paired(split)
-    pl.semaphore_wait(barrier, greeted)
-    pack_and_send(0)
-
-    for load in loads[2:]:
-        load.wait()
-    sources = [(stiff_ref, n, 1.0) for n in range(dims)]
-    sources += [(ref, n, -1.0) for ref in (own_ref, other_ref) for n in range(faces)]
-    for n in range(0, len(sources), 2):
-        some = jnp.concatenate([ref[k] * sign for ref, k, sign in sources[n : n + 2]], 0)
-        high = some.astype(bf16).astype(f32)
-        low = some - high
-        mats_ref[n * basis : n * basis + some.shape[0], :] = jnp.concatenate([high, high, low, low], 1).astype(bf16)
-
-    for f in range(faces):
+    pack(0)
+    pack(1)
+    loads[2].wait()
+
+    def build_hot(f):
         names = faces_ref[f : f + 1, :]
         own = hot_of(0, elements, names)
         hot_own[f, :elements, :] = own
@@ -250,6 +243,21 @@
                 at = (2 * begin + n) * half
                 hot_halo[f, at : at + half, :] = some
                 hot_halo[f, at + many * half : at + (many + 1) * half, :] = some
+
+    for f in range(faces):
+        build_hot(f)
+    pl.semaphore_wait(barrier, greeted)
+    start_slots(0, ORDER)
+    for load in loads[3:]:
+        load.wait()
+    sources = [(stiff_ref, n, 1.0) for n in range(dims)]
+    sources += [(ref, n, -1.0) for ref in (own_ref, other_ref) for n in range(faces)]
+    for n in range(0, len(sources), 2):
+        some = jnp.concatenate([ref[k] * sign for ref, k, sign in sources[n : n + 2]], 0)
+        high = some.astype(bf16).astype(f32)
+        low = some - high
+        mats_ref[n * basis : n * basis + some.shape[0], :] = jnp.concatenate([high, high, low, low], 1).astype(bf16)
+
     absent = jnp.full((1, LANES - receivers), -1, jnp.int32)
     hot = hot_of(0, elements, jnp.concatenate([element_ref[...], absent], 1))
     slot_row = jnp.concatenate([slot_ref[...], absent], 1).astype(f32)

time: 100 us -> 97.3 us (0.973)
  Pallas kernels: 98.4 us -> 95.7 us
    pallas_call x1, Pallas kernels: 96.1 us -> 93.4 us  [per_device(): pl.pallas_call(steps_kernel, out_shape=(jax.ShapeDtypeStruct((quantities,...]
where the time goes in v3:
time: 97.3 us; the launch traced here: 97.1 us
  Pallas kernels  95.7 us (98%)
  between operations  1.45 us (1%)
    pallas_call x1, Pallas kernels, per_device(): pl.pallas_call(steps_kernel, out_shape=(jax.ShapeDtypeStruct((quantities,...  93.4 us
    pallas_call x1, Pallas kernels, per_device(): pl.pallas_call(store_kernel, out_shape=tuple((jax.ShapeDtypeStruct(a.shap...  2.24 us

profile of v3, /device:TPU:0, one launch (start us, length us, event | category | flops | bytes accessed | tf_op | source)
XLA Modules:
  0.0 97.1 jit_solution(11624296614865219038)
XLA Ops:
  1.3 93.4 %steps.1 = (f32[9,56,640]{2,1,0:T(8,128)}, f32[1,3]{1,0:T(1,128)}, f32[9,3,16]{2,1,0:T(4,128)}) custom-call(s32[8,64]{1,0:T(8,128)} %bitcast.15, f32[9,56,640]{2,1,0:T(8,128)} %bitcast.10, s32[4,640]{1,0:T(4,128)} %faces_hbm.1, f32[3,56,56]{2,1,0:T(8,128)} %stiff_hbm.1, f32[4,56,56]{2,1,0:T(8,128)} %own_hbm.1, f32[4,56,56]{2,1,0:T(8,128)} %other_hbm.1, ...), custom_call_target="tpu_custom_call" | custom-call | tf_op jit(solution)/shard_map/steps/pallas_call | solution.py:536
  94.7 2.2 %store.1 = (f32[9,56,640]{2,1,0:T(8,128)}, f32[9,3,16]{2,1,0:T(4,128)}, f32[1,3]{1,0:T(1,128)}) custom-call(f32[9,56,640]{2,1,0:T(8,128)} %get-tuple-element.9.state_hbm, f32[9,3,16]{2,1,0:T(4,128)} %get-tuple-element.10.trace_hbm, f32[1,3]{1,0:T(1,128)} %get-tuple-element.11.energy_hbm), custom_call_target="tpu_custom_call" | custom-call | tf_op jit(solution)/shard_map/store/pallas_call | solution.py:577
